TPU v7x, 32 devices: a whole 2x2x4 slice. The times are simulated.
32 devices in a mesh: py: 8 (over y, x, core), pz: 4 (over z).
Axes of the slice: x: 2, y: 2, z: 4, core: 2. Of those that a mesh axis runs over, the one named last changes fastest.
Arguments:
- velocity: float32 [3, 320, 320, 320], P(None, 'py', 'pz'), may hold values from -12 to 12
Outputs:
- filtered_velocity: float32 [3, 128, 128, 128], P(None, 'py', 'pz')
- subgrid_stress: float32 [6, 128, 128, 128], P(None, 'py', 'pz')
All inputs are finite; a program needn't handle non-finite values.
Results may differ from a plain program's by a relative error of at most 0.000082.
Values sent between devices are 32-bit elements; how exact they have to be, the bound alone decides.
A program may use at most 128 MiB of HBM per device.

v0:
```python
import math

import jax
import jax.numpy as jnp
from jax import lax
from jax.sharding import PartitionSpec as P

N = 320
M = 128


highest = lax.Precision.HIGHEST
factor_pairs = ((0, 0), (0, 1), (0, 2), (1, 1), (1, 2), (2, 2))


def mode_values(length):
    positions = jnp.arange(length, dtype=jnp.int32)
    return jnp.where(positions < length // 2, positions, positions - length)


def angles(mode_list, sample_points, period):
    residues = jnp.mod(jnp.mod(mode_list, period)[None, :] * sample_points[:, None], period)
    return residues.astype(jnp.float32) * (2.0 * math.pi / period)


def complex_table(phases, direction):
    cosines = jnp.cos(phases)
    sine_values = direction * jnp.sin(phases)
    return jnp.stack(
        [jnp.stack([cosines, sine_values], axis=1), jnp.stack([-sine_values, cosines], axis=1)],
        axis=0,
    )


def shards(velocity):
    row_devices = lax.axis_size("py")
    column_devices = lax.axis_size("pz")
    row_place = lax.axis_index("py")
    column_place = lax.axis_index("pz")
    components = [velocity[component] for component in range(3)]
    fields = jnp.stack(
        components
        + [
            components[left_index] * components[right_index]
            for left_index, right_index in factor_pairs
        ]
    )
    signed_modes = mode_values(M)
    third_modes = jnp.arange(M // 2, dtype=jnp.int32)
    third_weight = jnp.where(third_modes == 0, 1.0, 2.0).astype(jnp.float32)
    third_count = third_modes.shape[0]
    third_block = third_count // row_devices
    first_block = M // column_devices
    second_coarse = M // row_devices
    fine_points = jnp.arange(N, dtype=jnp.int32)
    coarse_points = jnp.arange(M, dtype=jnp.int32)
    third_phase = angles(third_modes, fine_points, N)
    third_table = jnp.stack([jnp.cos(third_phase), -jnp.sin(third_phase)], axis=1)
    third_table = third_table.reshape(N, 2, row_devices, third_block)
    spread = jnp.einsum("fyzx,xapq->faypzq", fields, third_table, precision=highest)
    first_table = complex_table(angles(signed_modes, fine_points, N), -1.0)
    first_table = first_table.reshape(2, N, 2, column_devices, first_block)
    first_done = jnp.einsum(
        "nayozq,aybrs->nbrszq",
        lax.all_to_all(spread, "py", split_axis=3, concat_axis=2, tiled=True),
        first_table,
        precision=highest,
    )
    first_here = lax.dynamic_slice_in_dim(signed_modes, column_place * first_block, first_block)
    third_here = lax.dynamic_slice_in_dim(third_modes, row_place * third_block, third_block)
    nyquist = -(M // 2)
    retained = (
        (first_here != nyquist)[:, None, None]
        & (third_here != nyquist)[None, :, None]
        & (signed_modes != nyquist)[None, None, :]
    )
    wave_squares = (
        (first_here.astype(jnp.float32) ** 2)[:, None, None]
        + (third_here.astype(jnp.float32) ** 2)[None, :, None]
        + (signed_modes.astype(jnp.float32) ** 2)[None, None, :]
    )
    filter_width = 2.0 * math.pi / M
    filter_gain = jnp.where(
        retained, jnp.exp(-wave_squares * (filter_width * filter_width / 24.0)), 0.0
    )
    second_forward = complex_table(angles(signed_modes, fine_points, N), -1.0)
    second_inverse = complex_table(angles(signed_modes, coarse_points, M), 1.0)
    second_inverse = second_inverse.reshape(2, M, 2, row_devices, second_coarse)
    spectral = jnp.einsum(
        "naoszq,azbk->nbsqk",
        lax.all_to_all(first_done, "pz", split_axis=2, concat_axis=4, tiled=True),
        second_forward,
        precision=highest,
    )
    spectral = spectral * filter_gain[None, None]
    second_done = jnp.einsum("nasqk,akbpc->nbspcq", spectral, second_inverse, precision=highest)
    third_inverse = (
        complex_table(angles(third_modes, coarse_points, M).T, 1.0)
        * third_weight[None, :, None, None]
    )
    inverse_scale = 1.0 / float(N) ** 3
    first_phase = angles(signed_modes, coarse_points, M)
    first_inverse = jnp.stack([jnp.cos(first_phase), -jnp.sin(first_phase)], axis=0) * inverse_scale
    third_form = "nasocj,ajbx->nbscx"
    third_done = jnp.einsum(
        third_form,
        lax.all_to_all(second_done, "py", split_axis=3, concat_axis=5, tiled=True),
        third_inverse,
        precision=highest,
    )
    first_local = lax.dynamic_slice_in_dim(
        first_inverse, column_place * first_block, first_block, 1
    )
    summed = lax.psum_scatter(
        jnp.einsum("nascx,asy->xncy", third_done, first_local, precision=highest),
        "pz",
        scatter_dimension=0,
        tiled=True,
    )
    coarse = jnp.transpose(summed, (1, 2, 0, 3))
    filtered = coarse[:3]
    stress = jnp.stack(
        [
            coarse[3 + position] - coarse[left_index] * coarse[right_index]
            for position, (left_index, right_index) in enumerate(factor_pairs)
        ]
    )
    return (filtered, stress)


def solution(mesh):
    placed = (P(None, "py", "pz", None),)
    return jax.shard_map(
        shards,
        mesh=mesh,
        in_specs=placed,
        out_specs=(P(None, "py", "pz", None), P(None, "py", "pz", None)),
        check_vma=False,
    )
```

profile of v0, /device:TPU:0, one launch (start us, length us, event | category | flops | bytes accessed | tf_op | source)
XLA Modules:
  0.0 980.5 jit_solution(11421768916735628603)
XLA Ops:
  7.2 11.4 %constant_dynamic-update-slice_fusion = f32[9,40,80,320]{3,2,1,0:T(8,128)} fusion(f32[3,40,80,320]{3,2,1,0:T(8,128)} %param.1), kind=kLoop, calls=%fused_computation.131 | loop fusion | bytes 27033600
  18.5 4.9 multiply_dynamic-update-slice_fusion.5
  23.5 0.0 copy-start
  23.5 7.1 multiply_dynamic-update-slice_fusion.4
  30.5 2.8 copy-done
  33.3 2.7 multiply_dynamic-update-slice_fusion.3
  36.0 2.5 multiply_dynamic-update-slice_fusion.2
  38.5 2.7 multiply_dynamic-update-slice_fusion.1
  41.3 2.5 multiply_dynamic-update-slice_fusion
  43.8 0.5 fusion.57
  44.3 83.5 %fusion.6 = f32[9,2,40,8,80,8]{4,5,2,0,3,1:T(8,128)S(1)} fusion(f32[9,40,80,320]{3,2,1,0:T(8,128)} %multiply_dynamic-update-slice_fusion, f32[320,1,8,8]{0,3,2,1:T(8,128)S(1)} %get-tuple-element.22, f32[320,1,8,8]{0,3,2,1:T(8,128)S(1)} %get-tuple-element.21), kind=kOutput, calls=%fused_computation.7 | convolution fusion | flops 14155816960 | bytes 51773440 | tf_op jit(solution)/shard_map/fyzx,xapq->faypzq/dot_general | solution.py:60
  127.8 8.0 copy.13
  135.8 6.3 all-to-all-start
  142.2 0.9 sine_multiply_fusion
  143.0 256.8 %all-to-all-done = f32[9,2,40,8,80,8]{4,5,2,0,1,3:T(8,128)} async-done(((f32[9,2,40,8,80,8]{4,5,2,0,1,3:T(8,128)}), f32[9,2,40,8,80,8]{4,5,2,0,1,3:T(8,128)}, u32[]{:S(2)}, u32[]{:S(2)}) %all-to-all-start) | async-done | bytes 14745632 | tf_op jit(solution)/shard_map/all_to_all | solution.py:65
  399.8 9.3 copy.14
  409.2 29.3 %fusion.16 = f32[9,2,4,32,80,8]{4,3,5,0,2,1:T(8,128)} fusion(f32[9,2,320,80,8,1,1]{3,4,2,1,0,6,5:T(8,128)S(1)} %bitcast.122, f32[1,320,1,4,32]{1,4,0,3,2:T(8,128)S(1)} %get-tuple-element.25, f32[1,320,1,4,32]{1,4,0,3,2:T(8,128)S(1)} %get-tuple-element.24, f32[1,320,1,4,32]{1,4,0,3,2:T(8,128)S(1)} %get-tuple-element.23), kind=kOutput, calls=%fused_computation.20 | convolution fusion | flops 11325112320 | bytes 21135360 | tf_op jit(solution)/shard_map/nayozq,aybrs->nbrszq/dot_general | solution.py:63
  438.4 9.4 copy.16
  447.8 5.8 all-to-all-start.1
  453.7 0.1 convert_multiply_fusion.2
  453.8 0.1 broadcast_compare_fusion.2
  453.8 0.1 convert_multiply_fusion.1
  453.9 0.1 broadcast_compare_fusion.1
  454.0 0.7 sine_multiply_fusion.1
  454.8 0.1 broadcast_and_fusion
  454.9 0.1 broadcast_add_fusion
  454.9 0.1 exponential_select_fusion
  455.1 0.3 fusion.81
  455.4 201.8 %all-to-all-done.1 = f32[9,2,4,32,80,8]{4,3,5,0,1,2:T(8,128)} async-done(((f32[9,2,4,32,80,8]{4,3,5,0,1,2:T(8,128)}), f32[9,2,4,32,80,8]{4,3,5,0,1,2:T(8,128)}, u32[]{:S(2)}, u32[]{:S(2)}) %all-to-all-start.1) | async-done | bytes 5898272 | tf_op jit(solution)/shard_map/all_to_all | solution.py:91
  657.2 16.7 %copy.48 = f32[9,2,1,32,4,80,8]{5,4,3,1,6,0,2:T(4,128)} copy(f32[9,2,1,32,4,80,8]{5,3,6,0,1,4,2:T(8,128)} %bitcast.29) | data formatting | bytes 11796480 | tf_op jit(solution)/shard_map/naoszq,azbk->nbsqk/reduce_sum | solution.py:89
  673.9 10.9 %reshape.721 = f32[9,2,32,320,8,1]{3,2,1,4,0,5:T(8,128)} reshape(f32[9,2,1,32,4,80,8]{5,4,3,1,6,0,2:T(4,128)} %copy.48) | data formatting | bytes 11796480 | tf_op jit(solution)/shard_map/naoszq,azbk->nbsqk/reduce_sum | solution.py:89
  684.8 9.3 fusion.9
  694.1 7.8 convolution_bitcast_fusion
  701.9 4.8 copy.68
  706.7 9.0 reshape.733
  715.7 4.9 all-to-all-start.2
  720.7 0.2 reduce-scatter.2.cloned.1.call-start
  720.9 0.2 fusion.89
  721.2 0.3 sine_negate_fusion.1
  721.5 28.7 %all-to-all-done.2 = f32[8,1,73728]{2,1,0:T(1,128)S(1)} async-done(((f32[8,1,73728]{2,1,0:T(1,128)}), f32[8,1,73728]{2,1,0:T(1,128)S(1)}, u32[]{:S(2)}, u32[]{:S(2)}) %all-to-all-start.2) | async-done | bytes 2359328 | tf_op jit(solution)/shard_map/all_to_all | solution.py:107
  750.1 0.5 broadcast.1036
  750.6 8.6 reduce
  759.2 8.4 reshape.734
  767.6 4.9 bitcast_bitcast_fusion
  772.5 16.5 %fusion.4 = f32[2,128,9,32,16,1]{1,3,5,0,4,2:T(8,128)S(1)} fusion(f32[1,64,2,128]{3,1,0,2:T(8,128)S(1)} %get-tuple-element.17, f32[1,64,2,128]{3,1,0,2:T(8,128)S(1)} %get-tuple-element.16, f32[64]{0:T(128)S(1)} %compare_select_fusion.5, f32[9,2,32,1,16,8,8]{2,4,6,0,1,5,3:T(8,128)S(1)} %bitcast_bitcast_fusion), kind=kOutput, calls=%fused_computation.4 | convolution fusion | flops 1812004864 | bytes 7209216 | tf_op jit(solution)/shard_map/nasocj,ajbx->nbscx/dot_general | solution.py:105
  789.0 10.3 %fusion.13 = f32[128,9,16,128]{0,3,2,1:T(8,128)} fusion(f32[2,128,9,32,16,1]{1,3,5,0,4,2:T(8,128)S(1)} %fusion.4, s32[]{:T(128)S(6)} %select_n.292, f32[1,128,128]{2,1,0:T(8,128)S(1)} %get-tuple-element.27, f32[1,128,128]{2,1,0:T(8,128)S(1)} %get-tuple-element.26), kind=kOutput, calls=%fused_computation.19 | convolution fusion | flops 1811955712 | bytes 14286852 | tf_op jit(solution)/shard_map/nascx,asy->xncy/dot_general | solution.py:115
  799.3 9.7 copy.22
  809.0 0.0 reduce-scatter.2.cloned.1.call-update
  809.0 158.4 %reduce-scatter.2.cloned.1.call-done = f32[32,9,16,128]{3,2,1,0:T(8,128)} async-done(((f32[128,9,16,128]{3,2,1,0:T(8,128)}), f32[32,9,16,128]{3,2,1,0:T(8,128)}) %reduce-scatter.2.cloned.1.call-update) | async-done | bytes 2359312 | tf_op jit(solution)/shard_map/reduce_scatter | solution.py:114
  967.5 1.2 slice.62
  968.6 1.8 slice_subtract_fusion
  970.4 1.1 copy.29
  971.5 0.1 copy_dynamic-update-slice_fusion.5
  971.6 0.1 copy_dynamic-update-slice_fusion.4
  971.7 0.1 copy_dynamic-update-slice_fusion.3
  971.8 0.1 copy_dynamic-update-slice_fusion.2
  971.9 0.1 copy_dynamic-update-slice_fusion.1
  972.0 0.1 copy_dynamic-update-slice_fusion
  972.1 0.0 copy-start.1
  972.1 1.1 copy-done.1
  (12 shorter events, 0.1 us)
Async XLA Ops:
  23.5 9.8 %copy-start = (f32[3,40,80,320]{3,2,1,0:T(8,128)S(1)}, f32[3,40,80,320]{3,2,1,0:T(8,128)}, u32[]{:S(2)}) copy-start(f32[3,40,80,320]{3,2,1,0:T(8,128)} %param.1) | copy-start | bytes 36864004
  135.8 264.0 %all-to-all-start = ((f32[9,2,40,8,80,8]{4,5,2,0,1,3:T(8,128)}), f32[9,2,40,8,80,8]{4,5,2,0,1,3:T(8,128)}, u32[]{:S(2)}, u32[]{:S(2)}) async-start(f32[9,2,40,8,80,8]{4,5,2,0,1,3:T(8,128)} %copy.13), calls=%async_computation | async-start | bytes 47185920 | tf_op jit(solution)/shard_map/all_to_all | solution.py:65
  447.8 209.4 %all-to-all-start.1 = ((f32[9,2,4,32,80,8]{4,3,5,0,1,2:T(8,128)}), f32[9,2,4,32,80,8]{4,3,5,0,1,2:T(8,128)}, u32[]{:S(2)}, u32[]{:S(2)}) async-start(f32[9,2,4,32,80,8]{4,3,5,0,1,2:T(8,128)} %copy.16), calls=%async_computation.1 | async-start | bytes 18874368 | tf_op jit(solution)/shard_map/all_to_all | solution.py:91
  715.7 34.4 %all-to-all-start.2 = ((f32[8,1,73728]{2,1,0:T(1,128)}), f32[8,1,73728]{2,1,0:T(1,128)S(1)}, u32[]{:S(2)}, u32[]{:S(2)}) async-start(f32[8,1,73728]{2,1,0:T(1,128)} %reshape.733), calls=%async_computation.2 | async-start | bytes 4718592 | tf_op jit(solution)/shard_map/all_to_all | solution.py:107
  720.7 246.8 %reduce-scatter.2.cloned.1.call-start = ((), (), s32[]{:S(2)}) async-start(), calls=%async_computation.4 | async-start | bytes 11796480 | tf_op jit(solution)/shard_map/reduce_scatter | solution.py:114
  972.1 1.1 copy-start.1
Sparse Core Ops, SparseCore 0:
  809.1 158.2 reduce-scatter.1
where the time goes:
time: 985 us; the launch traced here: 980 us
  waiting for transfers between devices  646 us (66%)
  matrix products  157 us (16%)
  local copies, waits for them, and re-layouts  110 us (11%)
  other arithmetic  36.4 us (4%)
  starting transfers between devices  17.3 us (2%)
  between operations  14.7 us (1%)
    all_to_all x1, waiting for transfers between devices, shards(): lax.all_to_all(spread, 'py', split_axis=3, concat_axis=2, tiled=True)  257 us
    all_to_all x1, waiting for transfers between devices, shards(): lax.all_to_all(first_done, 'pz', split_axis=2, concat_axis=4, tiled=True)  202 us
    reduce_scatter x1, waiting for transfers between devices, shards(): lax.psum_scatter(jnp.einsum('nascx,asy->xncy', third_done, first_local, p...  158 us
    dot_general x1, matrix products, shards(): jnp.einsum('fyzx,xapq->faypzq', fields, third_table, precision=highest)  83.5 us
    unnamed x13, local copies, waits for them, and re-layouts  34.3 us
    dot_general x1, matrix products, shards(): jnp.einsum('nayozq,aybrs->nbrszq', lax.all_to_all(spread, 'py', split_axi...  29.3 us
    all_to_all x1, waiting for transfers between devices, shards(): lax.all_to_all(second_done, 'py', split_axis=3, concat_axis=5, tiled=True)  28.7 us
    reduce_sum x2, local copies, waits for them, and re-layouts, shards(): jnp.einsum('naoszq,azbk->nbsqk', lax.all_to_all(first_done, 'pz', split_a...  27.6 us
  transfers between devices with their start and end apart: 4, of which 4 were waited for; matrix products, arithmetic and copies ran while one was open for 0% of the time, Pallas kernels for 0%

commit v1 on v0

v1 whole, which is shorter than its diff:
```python
import math

import jax
import jax.numpy as jnp
import numpy as np
from jax import lax
from jax.sharding import PartitionSpec as P

factor_pairs = ((0, 0), (0, 1), (0, 2), (1, 1), (1, 2), (2, 2))


def line_filter(fine, coarse):
    half = coarse // 2
    modes = np.arange(1, half)
    width = 2.0 * math.pi / coarse
    gain = np.exp(-(modes.astype(np.float64) ** 2) * (width * width / 24.0))
    turns = np.arange(coarse)[:, None] * fine - np.arange(fine)[None, :] * coarse
    period = fine * coarse
    matrix = np.ones((coarse, fine))
    for mode, weight in zip(modes, gain):
        matrix += 2.0 * weight * np.cos(2.0 * math.pi * ((mode * turns) % period) / period)
    return (matrix / fine).astype(np.float32)


def shards(velocity):
    fine = velocity.shape[3]
    coarse_size = fine * 2 // 5
    matrix = jnp.asarray(line_filter(fine, coarse_size))
    components = [velocity[component] for component in range(3)]
    fields = jnp.stack(components + [components[a] * components[b] for a, b in factor_pairs])
    high = lax.Precision.HIGH
    third = jnp.einsum("fabk,mk->fabm", fields, matrix, precision=high)
    third = lax.all_to_all(third, "pz", split_axis=3, concat_axis=2, tiled=True)
    second = jnp.einsum("fabm,nb->fanm", third, matrix, precision=high)
    second = lax.all_to_all(second, "py", split_axis=2, concat_axis=1, tiled=True)
    coarse = jnp.einsum("fanm,pa->fnmp", second, matrix, precision=high)
    stress = jnp.stack(
        [coarse[3 + p] - coarse[a] * coarse[b] for p, (a, b) in enumerate(factor_pairs)]
    )
    return coarse[:3], stress


def solution(mesh):
    placed = P(None, "py", "pz", None)
    return jax.shard_map(
        shards, mesh=mesh, in_specs=(placed,), out_specs=(placed, placed), check_vma=False
    )
```

time: 985 us -> 978 us (level)
  waiting for transfers between devices: 646 us -> 0 us
  blocking collectives: 0 us -> 597 us
  local copies, waits for them, and re-layouts: 110 us -> 174 us
  other arithmetic: 36.4 us -> 87.6 us
  matrix products: 157 us -> 108 us
  starting transfers between devices: 17.3 us -> 0 us
  between operations: 14.7 us -> 1.14 us
    all_to_all x0 -> x2, blocking collectives: none -> 597 us  [the longest x1 525 us: shards(): third = lax.all_to_all(third, 'pz', split_axis=3, concat_axis=2, tiled=True)]
    all_to_all x3 -> x0, waiting for transfers between devices: 487 us -> none  [the longest x1 257 us: shards(): lax.all_to_all(spread, 'py', split_axis=3, concat_axis=2, tiled=True)]
    reduce_scatter x1 -> x0, waiting for transfers between devices: 158 us -> none  [shards(): lax.psum_scatter(jnp.einsum('nascx,asy->xncy', third_done, first_local, p...]
    dot_general x0 -> x2, local copies, waits for them, and re-layouts: none -> 55.6 us  [the longest x1 35.4 us: shards(): second = jnp.einsum('fabm,nb->fanm', third, matrix, precision=high)]
    all_to_all x1, other arithmetic: 8.61 us -> 64.1 us  [shards(): lax.all_to_all(second, 'py', split_axis=2, concat_axis=1, tiled=True)]
    dot_general x6 -> x3, matrix products: 157 us -> 108 us  [the longest x1 53.1 us: shards(): second = jnp.einsum('fabm,nb->fanm', third, matrix, precision=high)]
    all_to_all x3, local copies, waits for them, and re-layouts: 14.7 us -> 43.8 us  [the longest x2 22.5 us: shards(): lax.all_to_all(second, 'py', split_axis=2, concat_axis=1, tiled=True)]
    reduce_sum x2 -> x0, local copies, waits for them, and re-layouts: 27.6 us -> none  [shards(): jnp.einsum('naoszq,azbk->nbsqk', lax.all_to_all(first_done, 'pz', split_a...]
  transfers between devices with their start and end apart: 4 -> 0, of which waited for: 4 -> 0; matrix products, arithmetic and copies ran while one was open for 0% -> 0% of each run, Pallas kernels for 0% -> 0%
where the time goes in v1:
time: 978 us; the launch traced here: 968 us
  blocking collectives  597 us (61%)
  local copies, waits for them, and re-layouts  174 us (18%)
  matrix products  108 us (11%)
  other arithmetic  87.6 us (9%)
    all_to_all x1, blocking collectives, shards(): third = lax.all_to_all(third, 'pz', split_axis=3, concat_axis=2, tiled=True)  525 us
    all_to_all x1, blocking collectives, shards(): lax.all_to_all(second, 'py', split_axis=2, concat_axis=1, tiled=True)  72.4 us
    all_to_all x1, other arithmetic, shards(): lax.all_to_all(second, 'py', split_axis=2, concat_axis=1, tiled=True)  64.1 us
    unnamed x13, local copies, waits for them, and re-layouts  57.9 us
    dot_general x1, matrix products, shards(): second = jnp.einsum('fabm,nb->fanm', third, matrix, precision=high)  53.1 us
    dot_general x1, local copies, waits for them, and re-layouts, shards(): second = jnp.einsum('fabm,nb->fanm', third, matrix, precision=high)  35.4 us
    dot_general x1, matrix products, shards(): coarse = jnp.einsum('fanm,pa->fnmp', second, matrix, precision=high)  29.4 us
    dot_general x1, matrix products, shards(): third = jnp.einsum('fabk,mk->fabm', fields, matrix, precision=high)  25.2 us

profile of v1, /device:TPU:0, one launch (start us, length us, event | category | flops | bytes accessed | tf_op | source)
XLA Modules:
  0.0 968.2 jit_solution(8677616613082000563)
XLA Ops:
  0.6 11.4 %constant_dynamic-update-slice_fusion = f32[9,40,80,320]{3,2,1,0:T(8,128)} fusion(f32[3,40,80,320]{3,2,1,0:T(8,128)} %param.2), kind=kLoop, calls=%fused_computation.21 | loop fusion | bytes 27033600
  12.0 0.0 copy-start
  12.0 5.4 multiply_dynamic-update-slice_fusion.5
  17.4 7.3 multiply_dynamic-update-slice_fusion.4
  24.7 0.0 copy-done
  24.7 2.7 multiply_dynamic-update-slice_fusion.3
  27.4 2.5 multiply_dynamic-update-slice_fusion.2
  29.9 0.0 copy-start.3
  29.9 2.8 multiply_dynamic-update-slice_fusion.1
  32.7 2.5 multiply_dynamic-update-slice_fusion
  35.2 0.0 copy-done.3
  35.2 25.2 %fusion.8 = f32[9,40,80,128]{3,2,1,0:T(8,128)} fusion(f32[9,40,80,320]{3,2,1,0:T(8,128)} %multiply_dynamic-update-slice_fusion, f32[128,320,1,1]{0,1,3,2:T(8,128)S(1)} %copy-done.3), kind=kOutput, calls=%fused_computation.22 | convolution fusion | flops 7077888000 | bytes 51773440 | tf_op jit(solution)/shard_map/fabk,mk->fabm/dot_general | solution.py:32
  60.4 20.2 %copy.14 = f32[9,40,80,128]{2,1,0,3:T(8,128)} copy(f32[9,40,80,128]{3,2,1,0:T(8,128)} %fusion.8) | data formatting | bytes 29491200 | tf_op jit(solution)/shard_map/fabk,mk->fabm/dot_general | solution.py:32
  80.6 524.9 %all_to_all.36 = f32[9,40,80,128]{2,1,0,3:T(8,128)} all-to-all(f32[9,40,80,128]{2,1,0,3:T(8,128)} %copy.14), channel_id=1, replica_groups=mesh['py'=8,'pz'=4] {'pz'}, dimensions={3} | all-to-all | bytes 29491200 | tf_op jit(solution)/shard_map/all_to_all | solution.py:33
  605.5 21.3 %copy.15 = f32[9,40,80,128]{3,2,1,0:T(8,128)} copy(f32[9,40,80,128]{2,1,0,3:T(8,128)} %all_to_all.36) | data formatting | bytes 29491200 | tf_op jit(solution)/shard_map/all_to_all | solution.py:33
  626.8 0.0 copy-start.1
  626.8 35.4 %reshape.4 = f32[9,40,320,32]{3,2,1,0:T(8,128)} reshape(f32[9,40,80,128]{3,2,1,0:T(8,128)} %copy.15) | data formatting | bytes 29491200 | tf_op jit(solution)/shard_map/fabm,nb->fanm/dot_general | solution.py:34
  662.2 0.0 copy-done.1
  662.2 53.1 %convolution_bitcast_fusion = f32[9,40,128,32]{2,3,1,0:T(8,128)} fusion(f32[9,40,320,32]{3,2,1,0:T(8,128)} %reshape.4, f32[128,320,1,1]{0,1,3,2:T(8,128)S(1)} %copy-done.1), kind=kOutput, calls=%fused_computation.8 | convolution fusion | flops 2831155200 | bytes 20807680 | tf_op jit(solution)/shard_map/fabm,nb->fanm/dot_general | solution.py:34
  715.4 16.2 %copy.17 = f32[9,40,128,32]{1,3,0,2:T(8,128)} copy(f32[9,40,128,32]{2,3,1,0:T(8,128)} %convolution_bitcast_fusion) | data formatting | bytes 11796480 | tf_op jit(solution)/shard_map/fabm,nb->fanm/transpose | solution.py:34
  731.6 21.1 %reshape.15 = f32[8,1,184320]{2,1,0:T(1,128)} reshape(f32[128,9,32,40]{3,2,1,0:T(8,128)} %bitcast.22) | data formatting | bytes 11796480
  752.6 72.4 %all_to_all.37 = f32[8,1,184320]{2,1,0:T(1,128)} all-to-all(f32[8,1,184320]{2,1,0:T(1,128)} %reshape.15), channel_id=1, replica_groups=mesh['py'=8,'pz'=4] {'py'}, dimensions={0} | all-to-all | bytes 11796480 | tf_op jit(solution)/shard_map/all_to_all | solution.py:35
  825.1 0.5 broadcast
  825.6 64.1 %reduce = f32[8,184320]{1,0:T(8,128)} reduce(f32[8,1,184320]{2,1,0:T(1,128)} %all_to_all.37, f32[]{:T(128)} %broadcast), dimensions={1}, to_apply=%all_to_all.30.reduce_sub_computation | reduce | bytes 11796484 | tf_op jit(solution)/shard_map/all_to_all | solution.py:35
  889.7 24.3 %reshape.16 = f32[128,9,32,40]{3,2,1,0:T(8,128)} reshape(f32[8,184320]{1,0:T(8,128)} %reduce) | data formatting | bytes 11796480
  914.0 0.0 copy-start.2
  914.0 21.9 %copy.18 = f32[9,40,128,32]{3,2,1,0:T(8,128)} copy(f32[9,40,128,32]{1,3,0,2:T(8,128)} %bitcast.23) | data formatting | bytes 11796480 | tf_op jit(solution)/shard_map/all_to_all | solution.py:35
  935.9 0.0 copy-done.2
  935.9 29.4 %fusion = f32[9,16,32,128]{3,2,1,0:T(8,128)S(1)} fusion(f32[128,320,1,1]{0,1,3,2:T(8,128)S(1)} %copy-done.2, f32[9,320,16,32]{3,2,1,0:T(8,128)} %bitcast.21), kind=kOutput, calls=%fused_computation | convolution fusion | flops 1132462080 | bytes 8421376 | tf_op jit(solution)/shard_map/fanm,pa->fnmp/dot_general | solution.py:36
  965.4 0.9 slice.62
  966.3 0.1 fusion.6
  966.4 0.1 fusion.5
  966.5 0.1 fusion.3
  966.6 0.0 copy-start.4
  966.6 1.1 copy-done.4
  (3 shorter events, 0.1 us)
Async XLA Ops:
  12.0 12.7 %copy-start = (f32[3,40,80,320]{3,2,1,0:T(8,128)S(1)}, f32[3,40,80,320]{3,2,1,0:T(8,128)}, u32[]{:S(2)}) copy-start(f32[3,40,80,320]{3,2,1,0:T(8,128)} %param.2) | copy-start | bytes 36864004
  29.9 5.3 copy-start.3
  626.8 35.4 %copy-start.1 = (f32[128,320,1,1]{0,1,3,2:T(8,128)S(1)}, f32[128,320,1,1]{0,1,3,2:T(8,128)}, u32[]{:S(2)}) copy-start(f32[128,320,1,1]{0,1,3,2:T(8,128)} %constant.10) | copy-start | bytes 491524
  914.0 21.9 %copy-start.2 = (f32[128,320,1,1]{0,1,3,2:T(8,128)S(1)}, f32[128,320,1,1]{0,1,3,2:T(8,128)}, u32[]{:S(2)}) copy-start(f32[128,320,1,1]{0,1,3,2:T(8,128)} %constant.11) | copy-start | bytes 491524
  966.6 1.1 copy-start.4

commit v2 on v1

--- a/solution.py
+++ b/solution.py
@@ -1,12 +1,20 @@
+import functools
 import math
 
 import jax
 import jax.numpy as jnp
+import ml_dtypes
 import numpy as np
 from jax import lax
+from jax.experimental import pallas as pl
+from jax.experimental.pallas import tpu as pltpu
 from jax.sharding import PartitionSpec as P
 
+M = 128
+
 factor_pairs = ((0, 0), (0, 1), (0, 2), (1, 1), (1, 2), (2, 2))
+fields_count = 9
+LANES = 128
 
 
 def line_filter(fine, coarse):
@@ -22,13 +30,266 @@
     return (matrix / fine).astype(np.float32)
 
 
-def shards(velocity):
-    fine = velocity.shape[3]
-    coarse_size = fine * 2 // 5
-    matrix = jnp.asarray(line_filter(fine, coarse_size))
+def halves(matrix):
+    top = matrix.astype(ml_dtypes.bfloat16)
+    return top, (matrix - top.astype(np.float32)).astype(ml_dtypes.bfloat16)
+
+
+def split(value):
+    top = value.astype(jnp.bfloat16)
+    return top, (value - top.astype(jnp.float32)).astype(jnp.bfloat16)
+
+
+def dot(left, right):
+    return jnp.dot(left, right, preferred_element_type=jnp.float32)
+
+
+def rows_times(value, table):
+    width = table.shape[1] // 2
+    top, rest = split(value)
+    both = dot(top, table)
+    return both[:, :width] + both[:, width:] + dot(rest, table[:, :width])
+
+
+def kernel(
+    rows, columns, velocity, third, second, first, filtered, stress,
+    fine, lines, send_z, recv_z, send_y, recv_y, turned,
+    load_sem, send_z_sem, recv_z_sem, send_y_sem, recv_y_sem,
+):
+    me_y = lax.axis_index("py")
+    me_z = lax.axis_index("pz")
+    steps = fine.shape[1]
+    depth = fine.shape[3]
+    block = LANES // columns
+    band = filtered.shape[1]
+    MESH = pl.DeviceIdType.MESH
+
+    def load(c):
+        return pltpu.make_async_copy(velocity.at[c], fine.at[c], load_sem.at[c])
+
+    for c in range(3):
+        load(c).start()
+
+    barrier = pltpu.get_barrier_semaphore()
+    for k in range(1, columns):
+        pl.semaphore_signal(
+            barrier, inc=1, device_id=(me_y, (me_z + k) % columns), device_id_type=MESH
+        )
+    for j in range(1, rows):
+        pl.semaphore_signal(
+            barrier, inc=1, device_id=((me_y + j) % rows, me_z), device_id_type=MESH
+        )
+    pl.semaphore_wait(barrier, columns + rows - 2)
+
+    def copy_z(f, k):
+        return pltpu.make_async_remote_copy(
+            src_ref=send_z.at[f, k - 1],
+            dst_ref=recv_z.at[f, k],
+            send_sem=send_z_sem.at[f, k - 1],
+            recv_sem=recv_z_sem.at[f, k - 1],
+            device_id=(me_y, (me_z + k) % columns),
+            device_id_type=MESH,
+        )
+
+    def copy_y(f, j):
+        return pltpu.make_async_remote_copy(
+            src_ref=send_y.at[f, j - 1],
+            dst_ref=recv_y.at[f, pl.ds(j * steps, steps)],
+            send_sem=send_y_sem.at[f, j - 1],
+            recv_sem=recv_y_sem.at[f, j - 1],
+            device_id=((me_y + rows - j) % rows, me_z),
+            device_id_type=MESH,
+        )
+
+    def pair_of(f):
+        return f // 6 + f // 8, f - 3 - 2 * (f // 6) - f // 8
+
+    half = steps // 2
+
+    def contract_third(f, product):
+        if product:
+            left, right = pair_of(f)
+        else:
+            left = right = f
+
+        def piece(t, carry):
+            b, h = t // 2, t % 2
+            where = pl.ds(h * half, half)
+            value = fine[left, where, b]
+            if product:
+                value = value * fine[right, where, b]
+            value = value.reshape(half * depth, value.shape[-1])
+            out = rows_times(value, third[b])
+            lines[b, where] = out.reshape(half, depth, LANES)
+            return carry
+
+        lax.fori_loop(0, columns * 2, piece, 0)
+
+        def regroup(a, carry):
+            group = lax.broadcasted_iota(jnp.int32, (depth, LANES), 1) // block
+            parts = [lines[b, a] for b in range(columns)]
+            for k in range(columns):
+                out = parts[-1]
+                for b in range(columns - 1):
+                    out = jnp.where(group == (me_z + k + b) % columns, parts[b], out)
+                if k == 0:
+                    recv_z[f, 0, a] = out
+                else:
+                    send_z[f, k - 1, a] = out
+            return carry
+
+        lax.fori_loop(0, steps, regroup, 0)
+        for k in range(1, columns):
+            copy_z(f, k).start()
+
+    def contract_second(f):
+        for k in range(1, columns):
+            copy_z(f, k).wait_recv()
+
+        def piece(h, carry):
+            value = jnp.concatenate(
+                [recv_z[f, :, 2 * h + i].reshape(columns * depth, LANES) for i in range(2)], axis=1
+            )
+            top, rest = split(value)
+            table = second[...]
+            both = dot(table, top)
+            out = both[:M] + both[M:] + dot(table[:M], rest)
+            for i in range(2):
+                for j in range(rows):
+                    part = out[j * band : (j + 1) * band, i * LANES : (i + 1) * LANES]
+                    if j == 0:
+                        recv_y[f, 2 * h + i] = part
+                    else:
+                        send_y[f, j - 1, 2 * h + i] = part
+            return carry
+
+        lax.fori_loop(0, half, piece, 0)
+        for j in range(1, rows):
+            copy_y(f, j).start()
+
+    def contract_first(f, product):
+        for j in range(1, rows):
+            copy_y(f, j).wait_recv()
+        pad = jnp.zeros((LANES - rows * steps, LANES), jnp.float32)
+        for m in range(band):
+            plane = jnp.concatenate([recv_y[f, :, m, :], pad], axis=0).T
+            for g in range(columns):
+                turned[m * block : (m + 1) * block, g * LANES : (g + 1) * LANES] = plane[
+                    g * block : (g + 1) * block
+                ]
+        out = rows_times(turned[...], first[...]).reshape(band, block, M)
+        if product:
+            left, right = pair_of(f)
+            stress[f - 3] = out - filtered[left] * filtered[right]
+        else:
+            filtered[f] = out
+
+    def loop(start, stop, *work):
+        def body(f, carry):
+            for one in work:
+                one(f)
+            return carry
+
+        lax.fori_loop(start, stop, body, 0)
+
+    loop(0, 3, lambda f: load(f).wait(), lambda f: contract_third(f, False))
+    loop(3, fields_count, lambda f: contract_third(f, True))
+    loop(0, 2, contract_second)
+    loop(2, 5, contract_second, lambda f: contract_first(f - 2, False))
+    loop(5, fields_count, contract_second, lambda f: contract_first(f - 2, True))
+    loop(fields_count - 2, fields_count, lambda f: contract_first(f, True))
+
+    def finish(f):
+        for k in range(1, columns):
+            copy_z(f, k).wait_send()
+        for j in range(1, rows):
+            copy_y(f, j).wait_send()
+
+    loop(0, fields_count, finish)
+
+
+def tables(fine, rows, columns):
+    matrix = line_filter(fine, M)
+    block, band, depth = M // columns, M // rows, fine // columns
+    steps = fine // rows // columns
+    top, rest = halves(matrix)
+    third, second, first = [], [], []
+    for b in range(columns):
+        order = np.concatenate(
+            [np.arange(block) + ((g - b) % columns) * block for g in range(columns)]
+        )
+        third.append(np.concatenate([top.T[:, order], rest.T[:, order]], axis=1))
+    lines = np.concatenate([np.arange(band) + (-r % rows) * band for r in range(2 * rows)])
+    for z in range(columns):
+        order = np.concatenate(
+            [np.arange(depth) + ((z - k) % columns) * depth for k in range(columns)]
+        )
+        second.append(np.stack([half[lines][:, order] for half in (top, rest)]))
+        groups = []
+        for g in range(columns):
+            points = np.concatenate(
+                [
+                    (r % rows) * steps * columns + np.arange(steps) * columns + (g - z) % columns
+                    for r in range(2 * rows)
+                ]
+            )
+            groups.append(np.concatenate([top.T[points], rest.T[points]], axis=1))
+        first.append(np.stack(groups))
+    return np.stack(third), np.stack(second), np.stack(first)
+
+
+def kernel_shards(velocity):
+    rows, columns = lax.axis_size("py"), lax.axis_size("pz")
+    me_y, me_z = lax.axis_index("py"), lax.axis_index("pz")
+    _, lines, depth, fine = velocity.shape
+    steps = lines // columns
+    block, band = M // columns, M // rows
+    third, second, first = tables(fine, rows, columns)
+    second = lax.dynamic_slice(
+        jnp.asarray(second), (me_z, 0, (rows - me_y) % rows * band, 0), (1, 2, M, fine)
+    ).reshape(2 * M, fine)
+    first = lax.dynamic_slice(
+        jnp.asarray(first), (me_z, 0, me_y * steps, 0), (1, columns, rows * steps, 2 * M)
+    )[0]
+    first = jnp.pad(first, ((0, 0), (0, LANES - rows * steps), (0, 0)))
+    first = first.reshape(columns * LANES, 2 * M)
+    velocity = velocity.reshape(3, steps, columns, depth, fine)
+    vmem = pl.BlockSpec(memory_space=pltpu.VMEM)
+    dma = pltpu.SemaphoreType.DMA
+    f32 = jnp.float32
+    return pl.pallas_call(
+        functools.partial(kernel, rows, columns),
+        out_shape=(
+            jax.ShapeDtypeStruct((3, band, block, M), f32),
+            jax.ShapeDtypeStruct((6, band, block, M), f32),
+        ),
+        in_specs=[pl.BlockSpec(memory_space=pl.ANY), vmem, vmem, vmem],
+        out_specs=(vmem, vmem),
+        scratch_shapes=[
+            pltpu.VMEM((3, steps, columns, depth, fine), f32),
+            pltpu.VMEM((columns, steps, depth, LANES), f32),
+            pltpu.VMEM((fields_count, columns - 1, steps, depth, LANES), f32),
+            pltpu.VMEM((fields_count, columns, steps, depth, LANES), f32),
+            pltpu.VMEM((fields_count, rows - 1, steps, band, LANES), f32),
+            pltpu.VMEM((fields_count, rows * steps, band, LANES), f32),
+            pltpu.VMEM((band * block, columns * LANES), f32),
+            dma((3,)),
+            dma((fields_count, columns - 1)),
+            dma((fields_count, columns - 1)),
+            dma((fields_count, rows - 1)),
+            dma((fields_count, rows - 1)),
+        ],
+        compiler_params=pltpu.CompilerParams(
+            collective_id=0, has_side_effects=True, vmem_limit_bytes=67_000_000
+        ),
+    )(velocity, jnp.asarray(third), second, first)
+
+
+def plain_shards(velocity):
+    matrix = jnp.asarray(line_filter(velocity.shape[3], M))
     components = [velocity[component] for component in range(3)]
     fields = jnp.stack(components + [components[a] * components[b] for a, b in factor_pairs])
-    high = lax.Precision.HIGH
+    high = lax.Precision.HIGHEST
     third = jnp.einsum("fabk,mk->fabm", fields, matrix, precision=high)
     third = lax.all_to_all(third, "pz", split_axis=3, concat_axis=2, tiled=True)
     second = jnp.einsum("fabm,nb->fanm", third, matrix, precision=high)
@@ -40,6 +301,20 @@
     return coarse[:3], stress
 
 
+def shards(velocity):
+    rows, columns = lax.axis_size("py"), lax.axis_size("pz")
+    _, lines, depth, fine = velocity.shape
+    whole_tiles = (
+        M == LANES
+        and lines % (2 * columns) == 0
+        and depth % 16 == 0
+        and (M // rows) % 8 == 0
+        and (M // columns) % 8 == 0
+        and rows * (lines // columns) <= LANES
+    )
+    return kernel_shards(velocity) if whole_tiles else plain_shards(velocity)
+
+
 def solution(mesh):
     placed = P(None, "py", "pz", None)
     return jax.shard_map(

time: 978 us -> 348 us (0.36)
  blocking collectives: 597 us -> 0 us
  Pallas kernels: 0 us -> 334 us
  local copies, waits for them, and re-layouts: 174 us -> 6.65 us
  matrix products: 108 us -> 0 us
  other arithmetic: 87.6 us -> 0 us
    all_to_all x2 -> x0, blocking collectives: 597 us -> none  [the longest x1 525 us: shards(): third = lax.all_to_all(third, 'pz', split_axis=3, concat_axis=2, tiled=True)]
    pallas_call x0 -> x1, Pallas kernels: none -> 334 us  [kernel_shards(): pl.pallas_call(functools.partial(kernel, rows, columns), out_shape=(jax.S...]
    dot_general x3 -> x0, matrix products: 108 us -> none  [the longest x1 53.1 us: shards(): second = jnp.einsum('fabm,nb->fanm', third, matrix, precision=high)]
    all_to_all x1 -> x0, other arithmetic: 64.1 us -> none  [shards(): lax.all_to_all(second, 'py', split_axis=2, concat_axis=1, tiled=True)]
    dot_general x2 -> x0, local copies, waits for them, and re-layouts: 55.6 us -> none  [the longest x1 35.4 us: shards(): second = jnp.einsum('fabm,nb->fanm', third, matrix, precision=high)]
    unnamed x13 -> x4, local copies, waits for them, and re-layouts: 57.9 us -> 3.33 us
    all_to_all x3 -> x0, local copies, waits for them, and re-layouts: 43.8 us -> none  [the longest x2 22.5 us: shards(): lax.all_to_all(second, 'py', split_axis=2, concat_axis=1, tiled=True)]
    unnamed x10 -> x0, other arithmetic: 20.9 us -> none
where the time goes in v2:
time: 348 us; the launch traced here: 341 us
  Pallas kernels  334 us (96%)
  local copies, waits for them, and re-layouts  6.65 us (2%)
    pallas_call x1, Pallas kernels, kernel_shards(): pl.pallas_call(functools.partial(kernel, rows, columns), out_shape=(jax.S...  334 us

profile of v2, /device:TPU:0, one launch (start us, length us, event | category | flops | bytes accessed | tf_op | source)
XLA Modules:
  0.0 341.3 jit_solution(492242599271495125)
XLA Ops:
  0.6 1.0 dynamic-slice_bitcast_fusion
  1.6 0.7 pad.4
  2.4 1.6 constant_dynamic-slice_fusion
  4.0 333.9 %shard_map.59 = (f32[3,16,32,128]{3,2,1,0:T(8,128)}, f32[6,16,32,128]{3,2,1,0:T(8,128)}) custom-call(f32[3,10,4,80,320]{4,3,2,1,0:T(8,128)} %bitcast.5, bf16[4,320,256]{2,1,0:T(8,128)(2,1)} %constant.43.clone.third, bf16[256,320]{1,0:T(8,128)(2,1)} %bitcast.7, bf16[512,256]{1,0:T(8,128)(2,1)} %bitcast.6), custom_call_target="tpu_custom_call" | custom-call | tf_op jit(solution)/shard_map/pallas_call | solution.py:260
  337.9 0.0 copy-start
  337.9 2.2 copy.8
  340.1 0.0 copy-done
  340.1 1.1 copy.9
Async XLA Ops:
  337.9 2.2 copy-start

commit v3 on v2

--- a/solution.py
+++ b/solution.py
@@ -81,20 +81,20 @@
         )
     pl.semaphore_wait(barrier, columns + rows - 2)
 
-    def copy_z(f, k):
+    def copy_z(f, k, at=0, count=2):
         return pltpu.make_async_remote_copy(
-            src_ref=send_z.at[f, k - 1],
-            dst_ref=recv_z.at[f, k],
+            src_ref=send_z.at[f, k - 1, pl.ds(2 * at, count)],
+            dst_ref=recv_z.at[f, k, pl.ds(2 * at, count)],
             send_sem=send_z_sem.at[f, k - 1],
-            recv_sem=recv_z_sem.at[f, k - 1],
+            recv_sem=recv_z_sem.at[f, k - 1, at],
             device_id=(me_y, (me_z + k) % columns),
             device_id_type=MESH,
         )
 
-    def copy_y(f, j):
+    def copy_y(f, j, at=0, count=2):
         return pltpu.make_async_remote_copy(
-            src_ref=send_y.at[f, j - 1],
-            dst_ref=recv_y.at[f, pl.ds(j * steps, steps)],
+            src_ref=send_y.at[f, j - 1, pl.ds(2 * at, count)],
+            dst_ref=recv_y.at[f, pl.ds(j * steps + 2 * at, count)],
             send_sem=send_y_sem.at[f, j - 1],
             recv_sem=recv_y_sem.at[f, j - 1],
             device_id=((me_y + rows - j) % rows, me_z),
@@ -113,40 +113,41 @@
             left = right = f
 
         def piece(t, carry):
-            b, h = t // 2, t % 2
-            where = pl.ds(h * half, half)
+            u, b = t // columns, t % columns
+            where = pl.ds(2 * u, 2)
             value = fine[left, where, b]
             if product:
                 value = value * fine[right, where, b]
-            value = value.reshape(half * depth, value.shape[-1])
-            out = rows_times(value, third[b])
-            lines[b, where] = out.reshape(half, depth, LANES)
+            value = value.reshape(2 * depth, value.shape[-1])
+            lines[b] = rows_times(value, third[b]).reshape(2, depth, LANES)
             return carry
 
-        lax.fori_loop(0, columns * 2, piece, 0)
-
-        def regroup(a, carry):
+        def regroup(u, i):
             group = lax.broadcasted_iota(jnp.int32, (depth, LANES), 1) // block
-            parts = [lines[b, a] for b in range(columns)]
+            parts = [lines[b, i] for b in range(columns)]
             for k in range(columns):
                 out = parts[-1]
                 for b in range(columns - 1):
                     out = jnp.where(group == (me_z + k + b) % columns, parts[b], out)
                 if k == 0:
-                    recv_z[f, 0, a] = out
+                    recv_z[f, 0, 2 * u + i] = out
                 else:
-                    send_z[f, k - 1, a] = out
+                    send_z[f, k - 1, 2 * u + i] = out
+
+        def unit(u, carry):
+            lax.fori_loop(u * columns, (u + 1) * columns, piece, 0)
+            for i in range(2):
+                regroup(u, i)
+            for k in range(1, columns):
+                copy_z(f, k, u).start()
             return carry
 
-        lax.fori_loop(0, steps, regroup, 0)
-        for k in range(1, columns):
-            copy_z(f, k).start()
+        lax.fori_loop(0, half, unit, 0)
 
     def contract_second(f):
-        for k in range(1, columns):
-            copy_z(f, k).wait_recv()
-
         def piece(h, carry):
+            for k in range(1, columns):
+                copy_z(f, k, h).wait_recv()
             value = jnp.concatenate(
                 [recv_z[f, :, 2 * h + i].reshape(columns * depth, LANES) for i in range(2)], axis=1
             )
@@ -161,15 +162,15 @@
                         recv_y[f, 2 * h + i] = part
                     else:
                         send_y[f, j - 1, 2 * h + i] = part
+            for j in range(1, rows):
+                copy_y(f, j, h).start()
             return carry
 
         lax.fori_loop(0, half, piece, 0)
-        for j in range(1, rows):
-            copy_y(f, j).start()
 
     def contract_first(f, product):
         for j in range(1, rows):
-            copy_y(f, j).wait_recv()
+            copy_y(f, j, 0, steps).wait_recv()
         pad = jnp.zeros((LANES - rows * steps, LANES), jnp.float32)
         for m in range(band):
             plane = jnp.concatenate([recv_y[f, :, m, :], pad], axis=0).T
@@ -201,9 +202,9 @@
 
     def finish(f):
         for k in range(1, columns):
-            copy_z(f, k).wait_send()
+            copy_z(f, k, 0, steps).wait_send()
         for j in range(1, rows):
-            copy_y(f, j).wait_send()
+            copy_y(f, j, 0, steps).wait_send()
 
     loop(0, fields_count, finish)
 
@@ -267,7 +268,7 @@
         out_specs=(vmem, vmem),
         scratch_shapes=[
             pltpu.VMEM((3, steps, columns, depth, fine), f32),
-            pltpu.VMEM((columns, steps, depth, LANES), f32),
+            pltpu.VMEM((columns, 2, depth, LANES), f32),
             pltpu.VMEM((fields_count, columns - 1, steps, depth, LANES), f32),
             pltpu.VMEM((fields_count, columns, steps, depth, LANES), f32),
             pltpu.VMEM((fields_count, rows - 1, steps, band, LANES), f32),
@@ -275,7 +276,7 @@
             pltpu.VMEM((band * block, columns * LANES), f32),
             dma((3,)),
             dma((fields_count, columns - 1)),
-            dma((fields_count, columns - 1)),
+            dma((fields_count, columns - 1, steps // 2)),
             dma((fields_count, rows - 1)),
             dma((fields_count, rows - 1)),
         ],

time: 348 us -> 342 us (0.983); the launches traced: 341 us -> 342 us
  no operation moved by 1% of the time
where the time goes in v3:
time: 342 us
  Pallas kernels  334 us (98%)
  local copies, waits for them, and re-layouts  6.65 us (2%)
    pallas_call x1, Pallas kernels, kernel_shards(): pl.pallas_call(functools.partial(kernel, rows, columns), out_shape=(jax.S...  334 us

profile of v3, /device:TPU:0, one launch (start us, length us, event | category | flops | bytes accessed | tf_op | source)
XLA Modules:
  0.0 341.6 jit_solution(9517278539518396513)
XLA Ops:
  0.6 1.0 dynamic-slice_bitcast_fusion
  1.6 0.7 pad.4
  2.4 1.6 constant_dynamic-slice_fusion
  4.0 334.3 %shard_map.59 = (f32[3,16,32,128]{3,2,1,0:T(8,128)}, f32[6,16,32,128]{3,2,1,0:T(8,128)}) custom-call(f32[3,10,4,80,320]{4,3,2,1,0:T(8,128)} %bitcast.5, bf16[4,320,256]{2,1,0:T(8,128)(2,1)} %constant.43.clone.third, bf16[256,320]{1,0:T(8,128)(2,1)} %bitcast.7, bf16[512,256]{1,0:T(8,128)(2,1)} %bitcast.6), custom_call_target="tpu_custom_call" | custom-call | tf_op jit(solution)/shard_map/pallas_call | solution.py:261
  338.3 0.0 copy-start
  338.3 2.2 copy.8
  340.5 0.0 copy-done
  340.5 1.1 copy.9
Async XLA Ops:
  338.3 2.2 copy-start

commit v4 on v3

--- a/solution.py
+++ b/solution.py
@@ -67,8 +67,7 @@
     def load(c):
         return pltpu.make_async_copy(velocity.at[c], fine.at[c], load_sem.at[c])
 
-    for c in range(3):
-        load(c).start()
+    load(0).start()
 
     barrier = pltpu.get_barrier_semaphore()
     for k in range(1, columns):
@@ -193,7 +192,11 @@
 
         lax.fori_loop(start, stop, body, 0)
 
-    loop(0, 3, lambda f: load(f).wait(), lambda f: contract_third(f, False))
+    load(0).wait()
+    for c in range(1, 3):
+        load(c).start()
+    contract_third(0, False)
+    loop(1, 3, lambda f: load(f).wait(), lambda f: contract_third(f, False))
     loop(3, fields_count, lambda f: contract_third(f, True))
     loop(0, 2, contract_second)
     loop(2, 5, contract_second, lambda f: contract_first(f - 2, False))

time: 342 us -> 342 us (level)
  no operation moved by 1% of the time
where the time goes in v4:
time: 342 us
  Pallas kernels  334 us (98%)
  local copies, waits for them, and re-layouts  6.65 us (2%)
    pallas_call x1, Pallas kernels, kernel_shards(): pl.pallas_call(functools.partial(kernel, rows, columns), out_shape=(jax.S...  334 us

profile of v4, /device:TPU:0, one launch (start us, length us, event | category | flops | bytes accessed | tf_op | source)
XLA Modules:
  0.0 341.6 jit_solution(15667381028745489763)
XLA Ops:
  0.6 1.0 dynamic-slice_bitcast_fusion
  1.6 0.7 pad.4
  2.4 1.6 constant_dynamic-slice_fusion
  4.0 334.3 %shard_map.59 = (f32[3,16,32,128]{3,2,1,0:T(8,128)}, f32[6,16,32,128]{3,2,1,0:T(8,128)}) custom-call(f32[3,10,4,80,320]{4,3,2,1,0:T(8,128)} %bitcast.5, bf16[4,320,256]{2,1,0:T(8,128)(2,1)} %constant.43.clone.third, bf16[256,320]{1,0:T(8,128)(2,1)} %bitcast.7, bf16[512,256]{1,0:T(8,128)(2,1)} %bitcast.6), custom_call_target="tpu_custom_call" | custom-call | tf_op jit(solution)/shard_map/pallas_call | solution.py:264
  338.3 0.0 copy-start
  338.3 2.2 copy.8
  340.5 0.0 copy-done
  340.5 1.1 copy.9
Async XLA Ops:
  338.3 2.2 copy-start
